TPU v7x, 32 devices: a whole 2x2x4 slice. The times are simulated.
32 devices in a mesh: blk: 16 (over z, x, core), rep: 2 (over y).
Axes of the slice: x: 2, y: 2, z: 4, core: 2. Of those that a mesh axis runs over, the one named last changes fastest.
Arguments:
- measured: float32 [3, 16, 8, 1536], P(None, 'blk', None, 'rep'), may hold values from -4 to 4
- rot_vector: float32 [3, 16, 8, 1536], P(None, 'blk', None, 'rep'), may hold values from -6 to 6
- confidence: float32 [3, 16, 8, 1536], P(None, 'blk', None, 'rep'), may hold values from 0.5 to 2
- first_local: int32 [16, 8, 1536], P('blk', None, 'rep'), may hold values from 0 to 2047
- second_local: int32 [16, 8, 1536], P('blk', None, 'rep'), may hold values from 0 to 2047
- edge_counts: int32 [16, 8, 2], P('blk', None, 'rep'), may hold values from 256 to 768, as said below
- start_angles: float32 [3, 32768], P(None, 'blk'), may hold values from -4 to 4
- anchor: float32 [32768], P('blk'), may hold values from 0.05 to 0.5
Outputs:
- estimate: float32 [3, 32768], P(None, 'blk')
- weights: float32 [16, 8, 1536], P('blk', None, 'rep')
Inputs may be any that keep to these rules, and one draw needn't show every extreme that they name: `edge_counts`: live edges of a tile pair on one device fill its first slots; in every tile some pair holds 768 live edges on one device.
All inputs are finite; a program needn't handle non-finite values.
Results may differ from a plain program's by a relative error of at most 0.0001.
Values sent between devices are 32-bit elements; how exact they have to be, the bound alone decides.
No kernel may reach another device: no remote copies, remote signals or barrier semaphores. Data moves between devices by JAX's collectives and lax.ppermute only.
A program may use at most 128 MiB of HBM per device.

v0:
```python
import jax
import jax.numpy as jnp
from jax import lax
from jax.sharding import PartitionSpec as P

PASSES = 2
ITERS = 2
PAIRS = ((0, 0), (0, 1), (0, 2), (1, 1), (1, 2), (2, 2))
LOOKUP = ((0, 1, 2), (1, 3, 4), (2, 4, 5))
SOFTEN = 0.05


def shifted(value, axis, steps):
    count = lax.axis_size(axis)
    pairs = [(source, (source + steps) % count) for source in range(count)]
    return lax.ppermute(value, axis, pairs)


def rotations(vector):
    squared = vector[0] * vector[0] + vector[1] * vector[1] + vector[2] * vector[2]
    factor = 2.0 / (1.0 + squared)
    zeros = jnp.zeros_like(squared)
    skewed = (
        (zeros, -vector[2], vector[1]),
        (vector[2], zeros, -vector[0]),
        (-vector[1], vector[0], zeros),
    )
    matrix_rows = []
    for first in range(3):
        entries = []
        for second in range(3):
            term = skewed[first][second] + vector[first] * vector[second]
            if first == second:
                entries.append(1.0 + factor * (term - squared))
            else:
                entries.append(factor * term)
        matrix_rows.append(jnp.stack(entries))
    return jnp.stack(matrix_rows)


def rotate(rotation, vector):
    return jnp.sum(rotation * vector[None], axis=1)


def rotate_back(rotation, vector):
    return jnp.sum(rotation * vector[:, None], axis=0)


def block_parts(weighted, rotation):
    far_list = []
    near_list = []
    for first, second in PAIRS:
        near_list.append(jnp.sum(rotation[:, first] * weighted * rotation[:, second], axis=0))
        if first == second:
            far_list.append(weighted[first])
        else:
            far_list.append(jnp.zeros_like(weighted[0]))
    return (jnp.stack(far_list), jnp.stack(near_list))


def inverse_apply(blocks, vector):
    adjugate = jnp.stack(
        [
            blocks[3] * blocks[5] - blocks[4] * blocks[4],
            blocks[2] * blocks[4] - blocks[1] * blocks[5],
            blocks[1] * blocks[4] - blocks[2] * blocks[3],
            blocks[0] * blocks[5] - blocks[2] * blocks[2],
            blocks[1] * blocks[2] - blocks[0] * blocks[4],
            blocks[0] * blocks[3] - blocks[1] * blocks[1],
        ]
    )
    determinant = blocks[0] * adjugate[0] + blocks[1] * adjugate[1] + blocks[2] * adjugate[2]
    result = []
    for first in range(3):
        total = (
            adjugate[LOOKUP[first][0]] * vector[0]
            + adjugate[LOOKUP[first][1]] * vector[1]
            + adjugate[LOOKUP[first][2]] * vector[2]
        )
        result.append(total / determinant)
    return jnp.stack(result)


def spread(terms, index, total):
    return jax.vmap(lambda values: jax.ops.segment_sum(values, index, num_segments=total))(terms)


def on_device(
    measured, rot_vector, confidence, first_local, second_local, edge_counts, start_angles, anchor
):
    tile_cams = start_angles.shape[1]
    pair_count = first_local.shape[1]
    slot_count = first_local.shape[2]
    window_span = pair_count * tile_cams
    first = first_local.reshape(-1)
    second = (
        jnp.arange(pair_count, dtype=jnp.int32)[:, None] * tile_cams + second_local[0]
    ).reshape(-1)
    live = (
        (jnp.arange(slot_count, dtype=jnp.int32)[None, :] < edge_counts[0])
        .astype(jnp.float32)
        .reshape(-1)
    )
    measured = measured.reshape(3, -1)
    confidence = confidence.reshape(3, -1)
    rotation = rotations(rot_vector.reshape(3, -1))
    diagonal = jnp.stack(
        [anchor if first_c == second_c else jnp.zeros_like(anchor) for first_c, second_c in PAIRS]
    )

    def window_of(field):
        window = field
        width = 1
        while width < pair_count:
            ahead = shifted(window, "blk", -width)
            window = jnp.concatenate([window, ahead], axis=1)
            width = width * 2
        return window

    def returned(far_sums):
        current = far_sums
        width = pair_count
        while width > 1:
            half_width = width // 2
            moved = shifted(current[:, half_width:width], "blk", half_width)
            current = current[:, :half_width] + moved
            width = half_width
        return current[:, 0]

    def reduce_halves(sums):
        return lax.psum(sums, "rep")

    def collect(far_terms, near_terms):
        channels = far_terms.shape[0]
        far_sums = spread(far_terms, second, window_span).reshape(channels, pair_count, tile_cams)
        near_sums = spread(near_terms, first, tile_cams)
        return reduce_halves(returned(far_sums) + near_sums)

    def precond_sum(residual, scaled):
        return lax.psum(jnp.sum(residual * scaled), "blk")

    estimate = start_angles
    weights = live
    for sweep_index in range(PASSES):
        window = window_of(estimate)
        misfit = measured - (window[:, second] - rotate(rotation, estimate[:, first]))
        weights = live / jnp.sqrt(jnp.sum(confidence * misfit * misfit, axis=0) + SOFTEN * SOFTEN)
        weighted = weights * confidence
        terms = weighted * misfit
        far_part, near_part = block_parts(weighted, rotation)
        near_terms = jnp.concatenate([-rotate_back(rotation, terms), near_part], axis=0)
        far_terms = jnp.concatenate([terms, far_part], axis=0)
        totals = collect(far_terms, near_terms)
        residual = totals[:3] - anchor * estimate
        blocks = totals[3:] + diagonal
        scaled = inverse_apply(blocks, residual)
        direction = scaled
        norm_now = precond_sum(residual, scaled)
        for inner_index in range(ITERS):
            window = window_of(direction)
            changed = window[:, second] - rotate(rotation, direction[:, first])
            pushed = weighted * changed
            image = collect(pushed, -rotate_back(rotation, pushed)) + anchor * direction
            step_size = norm_now / lax.psum(jnp.sum(direction * image), "blk")
            estimate = estimate + step_size * direction
            residual = residual - step_size * image
            if inner_index + 1 < ITERS:
                scaled = inverse_apply(blocks, residual)
                norm_next = precond_sum(residual, scaled)
                direction = scaled + norm_next / norm_now * direction
                norm_now = norm_next
    return (estimate, weights.reshape(1, pair_count, slot_count))


def solution(mesh):
    return jax.shard_map(
        on_device,
        mesh=mesh,
        in_specs=(
            P(None, "blk", None, "rep"),
            P(None, "blk", None, "rep"),
            P(None, "blk", None, "rep"),
            P("blk", None, "rep"),
            P("blk", None, "rep"),
            P("blk", None, "rep"),
            P(None, "blk"),
            P("blk"),
        ),
        out_specs=(P(None, "blk"), P("blk", None, "rep")),
        check_vma=False,
    )
```

profile of v0, /device:TPU:0, one launch (start us, length us, event | category | flops | bytes accessed | tf_op | source)
XLA Modules:
  0.0 1505.5 jit_solution(13354158175996071067)
XLA Ops:
  7.2 5.5 collective-permute-start
  16.6 17.3 %gather_fusion.1 = f32[6144,3]{1,0:T(8,128)S(1)} fusion(f32[3,2048]{0,1:T(8,128)} %copy.781, s32[6144]{0:T(1024)S(1)} %broadcast_clamp_fusion), kind=kCustom, calls=%fused_computation.1 | custom fusion | bytes 172032 | tf_op jit(solution)/shard_map/gather | solution.py:146
  59.1 5.1 copy.780
  64.2 24.3 %gather_fusion = f32[6144,3]{1,0:T(8,128)} fusion(f32[3,16384]{0,1:T(8,128)} %copy.780, s32[6144]{0:T(1024)S(1)} %broadcast_clamp_fusion.1), kind=kCustom, calls=%fused_computation | custom fusion | bytes 172032 | tf_op jit(solution)/shard_map/gather | solution.py:146
  95.9 9.5 fusion.12
  105.4 5.4 fusion.44
  132.0 37.4 %scatter_custom_fusion = f32[9,16384]{0,1:T(8,128)} fusion(s32[6144]{0:T(1024)} %bitcast.235, f32[6144,9]{1,0:T(8,128)} %copy.791, f32[]{:T(128)} %constant.7.clone.1), kind=kCustom, calls=%fused_computation.39 | custom fusion | flops 55296 | bytes 590336 | tf_op jit(solution)/shard_map/vmap()/scatter-add | solution.py:85
  169.4 7.4 fusion.42
  185.3 4.2 collective-permute-done.3
  191.4 4.7 collective-permute-start.4
  213.9 32.3 %scatter_fusion = f32[9,2048]{0,1:T(8,128)} fusion(f32[9,2048]{0,1:T(8,128)} %bitcast.191, s32[6144]{0:T(1024)S(1)} %reshape.813, f32[6144,9]{1,0:T(8,128)} %copy.799), kind=kCustom, calls=%fused_computation.13 | custom fusion | flops 55296 | bytes 688128 | tf_op jit(solution)/shard_map/vmap()/scatter-add | solution.py:85
  251.1 20.2 %all-reduce.5.cloned.1.call-done = f32[9,2048]{1,0:T(8,128)} async-done(((f32[9,2048]{1,0:T(8,128)}), f32[9,2048]{1,0:T(8,128)}) %all-reduce.5.cloned.1.call-update) | async-done | bytes 73744 | tf_op jit(solution)/shard_map/psum | solution.py:131
  283.4 22.1 %gather_fusion.3 = f32[6144,3]{1,0:T(8,128)} fusion(f32[3,2048]{0,1:T(8,128)} %copy.802, s32[6144]{0:T(1024)S(1)} %broadcast_clamp_fusion), kind=kCustom, calls=%fused_computation.3 | custom fusion | bytes 172032 | tf_op jit(solution)/shard_map/gather | solution.py:161
  317.3 5.7 copy.801
  323.0 24.3 %gather_fusion.2 = f32[6144,3]{1,0:T(8,128)} fusion(f32[3,16384]{0,1:T(8,128)} %copy.801, s32[6144]{0:T(1024)S(1)} %broadcast_clamp_fusion.1), kind=kCustom, calls=%fused_computation.2 | custom fusion | bytes 172032 | tf_op jit(solution)/shard_map/gather | solution.py:161
  347.3 5.0 fusion.21
  352.2 34.2 %scatter_custom_fusion.2 = f32[3,16384]{0,1:T(8,128)} fusion(s32[6144]{0:T(1024)} %bitcast.236, f32[]{:T(128)} %constant.7.clone.1, f32[3,6144]{0,1:T(8,128)} %fusion.21), kind=kCustom, calls=%fused_computation.35 | custom fusion | flops 18432 | bytes 3342848 | tf_op jit(solution)/shard_map/vmap()/scatter-add | solution.py:85
  386.4 7.4 fusion.41
  408.3 4.8 collective-permute-done.10
  424.2 32.3 %scatter_fusion.1 = f32[3,2048]{0,1:T(8,128)} fusion(f32[3,2048]{0,1:T(8,128)} %bitcast.194, s32[6144]{0:T(1024)S(1)} %reshape.813, f32[6144,3]{1,0:T(8,128)} %copy.809), kind=kCustom, calls=%fused_computation.15 | custom fusion | flops 18432 | bytes 245760 | tf_op jit(solution)/shard_map/vmap()/scatter-add | solution.py:85
  458.6 8.6 psum.100
  468.7 30.2 %all-reduce.1 = (f32[]{:T(128)}, f32[]{:T(128)}) all-reduce(f32[]{:T(128)} %get-tuple-element.31, f32[]{:T(128)} %get-tuple-element.30), channel_id=1, replica_groups=mesh['blk'=16,'rep'=2] {'blk'}, use_global_device_ids=true, to_apply=%region_13.0 | all-reduce | flops 2 | bytes 16 | tf_op jit(solution)/shard_map/psum | solution.py:140
  504.2 30.1 %psum.102 = f32[]{:T(128)} all-reduce(f32[]{:T(128)} %multiply_reduce_fusion.17), channel_id=1, replica_groups=mesh['blk'=16,'rep'=2] {'blk'}, use_global_device_ids=true, to_apply=%region_22.0 | all-reduce | flops 1 | bytes 8 | tf_op jit(solution)/shard_map/psum | solution.py:140
  540.8 22.1 %gather_fusion.5 = f32[6144,3]{1,0:T(8,128)} fusion(f32[3,2048]{0,1:T(8,128)} %copy.811, s32[6144]{0:T(1024)S(1)} %broadcast_clamp_fusion), kind=kCustom, calls=%fused_computation.5 | custom fusion | bytes 172032 | tf_op jit(solution)/shard_map/gather | solution.py:161
  580.7 8.2 pad_maximum_fusion
  588.8 24.3 %gather_fusion.4 = f32[6144,3]{1,0:T(8,128)} fusion(f32[3,16384]{0,1:T(8,128)} %pad_maximum_fusion, s32[6144]{0:T(1024)S(1)} %broadcast_clamp_fusion.1), kind=kCustom, calls=%fused_computation.4 | custom fusion | bytes 172032 | tf_op jit(solution)/shard_map/gather | solution.py:161
  613.1 5.0 fusion.19
  618.1 34.2 %scatter_custom_fusion.4 = f32[3,16384]{0,1:T(8,128)} fusion(s32[6144]{0:T(1024)} %bitcast.237, f32[]{:T(128)} %constant.7.clone.1, f32[3,6144]{0,1:T(8,128)} %fusion.19), kind=kCustom, calls=%fused_computation.33 | custom fusion | flops 18432 | bytes 3342848 | tf_op jit(solution)/shard_map/vmap()/scatter-add | solution.py:85
  652.3 7.4 fusion.40
  673.1 5.6 collective-permute-done.16
  685.2 33.9 %scatter_fusion.2 = f32[3,2048]{0,1:T(8,128)S(1)} fusion(f32[3,2048]{0,1:T(8,128)S(1)} %bitcast.195, s32[6144]{0:T(1024)S(1)} %reshape.813, f32[6144,3]{1,0:T(8,128)} %copy.822), kind=kCustom, calls=%fused_computation.17 | custom fusion | flops 18432 | bytes 245760 | tf_op jit(solution)/shard_map/vmap()/scatter-add | solution.py:85
  719.4 8.3 psum.103
  728.5 30.3 %psum.104 = f32[]{:T(128)} all-reduce(f32[]{:T(128)} %multiply_reduce_fusion.16), channel_id=1, replica_groups=mesh['blk'=16,'rep'=2] {'blk'}, use_global_device_ids=true, to_apply=%region_29.0 | all-reduce | flops 1 | bytes 8 | tf_op jit(solution)/shard_map/psum | solution.py:164
  762.2 20.9 %gather_fusion.7 = f32[6144,3]{1,0:T(8,128)} fusion(f32[3,2048]{0,1:T(8,128)S(1)} %copy.824, s32[6144]{0:T(1024)S(1)} %broadcast_clamp_fusion), kind=kCustom, calls=%fused_computation.7 | custom fusion | bytes 172032 | tf_op jit(solution)/shard_map/gather | solution.py:146
  795.8 8.9 pad_maximum_fusion.1
  804.7 24.3 %gather_fusion.6 = f32[6144,3]{1,0:T(8,128)} fusion(f32[3,16384]{0,1:T(8,128)} %pad_maximum_fusion.1, s32[6144]{0:T(1024)S(1)} %broadcast_clamp_fusion.1), kind=kCustom, calls=%fused_computation.6 | custom fusion | bytes 172032 | tf_op jit(solution)/shard_map/gather | solution.py:146
  837.0 9.7 fusion.13
  848.8 5.2 fusion.43
  872.6 37.2 %scatter_custom_fusion.6 = f32[9,16384]{0,1:T(8,128)} fusion(s32[6144]{0:T(1024)} %bitcast.238, f32[6144,9]{1,0:T(8,128)} %copy.836, f32[]{:T(128)} %constant.7.clone.1), kind=kCustom, calls=%fused_computation.37 | custom fusion | flops 55296 | bytes 590336 | tf_op jit(solution)/shard_map/vmap()/scatter-add | solution.py:85
  909.8 7.4 fusion.39
  935.0 4.2 collective-permute-done.22
  953.1 32.3 %scatter_fusion.3 = f32[9,2048]{0,1:T(8,128)} fusion(f32[9,2048]{0,1:T(8,128)} %bitcast.192, s32[6144]{0:T(1024)S(1)} %reshape.813, f32[6144,9]{1,0:T(8,128)} %copy.841), kind=kCustom, calls=%fused_computation.19 | custom fusion | flops 55296 | bytes 688128 | tf_op jit(solution)/shard_map/vmap()/scatter-add | solution.py:85
  987.7 20.7 %all-reduce.7.cloned.1.call-done = f32[9,2048]{1,0:T(8,128)} async-done(((f32[9,2048]{1,0:T(8,128)}), f32[9,2048]{1,0:T(8,128)}) %all-reduce.7.cloned.1.call-update) | async-done | bytes 73744 | tf_op jit(solution)/shard_map/psum | solution.py:131
  1020.4 22.1 %gather_fusion.9 = f32[6144,3]{1,0:T(8,128)} fusion(f32[3,2048]{0,1:T(8,128)} %copy.844, s32[6144]{0:T(1024)S(1)} %broadcast_clamp_fusion), kind=kCustom, calls=%fused_computation.9 | custom fusion | bytes 172032 | tf_op jit(solution)/shard_map/gather | solution.py:161
  1054.1 5.7 copy.843
  1059.8 24.3 %gather_fusion.8 = f32[6144,3]{1,0:T(8,128)} fusion(f32[3,16384]{0,1:T(8,128)} %copy.843, s32[6144]{0:T(1024)S(1)} %broadcast_clamp_fusion.1), kind=kCustom, calls=%fused_computation.8 | custom fusion | bytes 172032 | tf_op jit(solution)/shard_map/gather | solution.py:161
  1084.0 5.0 fusion.17
  1089.0 34.2 %scatter_custom_fusion.8 = f32[3,16384]{0,1:T(8,128)} fusion(s32[6144]{0:T(1024)} %bitcast.239, f32[]{:T(128)} %constant.7.clone.1, f32[3,6144]{0,1:T(8,128)} %fusion.17), kind=kCustom, calls=%fused_computation.31 | custom fusion | flops 18432 | bytes 3342848 | tf_op jit(solution)/shard_map/vmap()/scatter-add | solution.py:85
  1123.2 7.4 fusion.38
  1145.0 4.8 collective-permute-done.28
  1160.9 32.3 %scatter_fusion.4 = f32[3,2048]{0,1:T(8,128)} fusion(f32[3,2048]{0,1:T(8,128)} %bitcast.196, s32[6144]{0:T(1024)S(1)} %reshape.813, f32[6144,3]{1,0:T(8,128)} %copy.851), kind=kCustom, calls=%fused_computation.21 | custom fusion | flops 18432 | bytes 245760 | tf_op jit(solution)/shard_map/vmap()/scatter-add | solution.py:85
  1195.3 8.6 psum.107
  1205.4 30.2 %all-reduce = (f32[]{:T(128)}, f32[]{:T(128)}) all-reduce(f32[]{:T(128)} %get-tuple-element.29, f32[]{:T(128)} %get-tuple-element.28), channel_id=1, replica_groups=mesh['blk'=16,'rep'=2] {'blk'}, use_global_device_ids=true, to_apply=%region_43.0 | all-reduce | flops 2 | bytes 16 | tf_op jit(solution)/shard_map/psum | solution.py:140
  1241.0 30.2 %psum.109 = f32[]{:T(128)} all-reduce(f32[]{:T(128)} %multiply_reduce_fusion.13), channel_id=1, replica_groups=mesh['blk'=16,'rep'=2] {'blk'}, use_global_device_ids=true, to_apply=%region_52.0 | all-reduce | flops 1 | bytes 8 | tf_op jit(solution)/shard_map/psum | solution.py:140
  1277.9 22.1 %gather_fusion.11 = f32[6144,3]{1,0:T(8,128)} fusion(f32[3,2048]{0,1:T(8,128)} %copy.853, s32[6144]{0:T(1024)S(1)} %broadcast_clamp_fusion), kind=kCustom, calls=%fused_computation.11 | custom fusion | bytes 172032 | tf_op jit(solution)/shard_map/gather | solution.py:161
  1317.8 8.2 pad_maximum_fusion.2
  1326.0 24.3 %gather_fusion.10 = f32[6144,3]{1,0:T(8,128)} fusion(f32[3,16384]{0,1:T(8,128)} %pad_maximum_fusion.2, s32[6144]{0:T(1024)S(1)} %broadcast_clamp_fusion.1), kind=kCustom, calls=%fused_computation.10 | custom fusion | bytes 172032 | tf_op jit(solution)/shard_map/gather | solution.py:161
  1350.3 5.0 fusion.15
  1355.2 34.2 %scatter_custom_fusion.10 = f32[3,16384]{0,1:T(8,128)} fusion(s32[6144]{0:T(1024)} %bitcast.240, f32[]{:T(128)} %constant.7.clone.1, f32[3,6144]{0,1:T(8,128)} %fusion.15), kind=kCustom, calls=%fused_computation.29 | custom fusion | flops 18432 | bytes 3342848 | tf_op jit(solution)/shard_map/vmap()/scatter-add | solution.py:85
  1389.4 7.4 fusion.37
  1410.3 5.6 collective-permute-done.34
  1422.3 33.9 %scatter_fusion.5 = f32[3,2048]{0,1:T(8,128)S(1)} fusion(f32[3,2048]{0,1:T(8,128)S(1)} %bitcast.193, s32[6144]{0:T(1024)S(1)} %reshape.813, f32[6144,3]{1,0:T(8,128)} %copy.864), kind=kCustom, calls=%fused_computation.23 | custom fusion | flops 18432 | bytes 245760 | tf_op jit(solution)/shard_map/vmap()/scatter-add | solution.py:85
  1456.6 8.3 psum.110
  1466.3 30.1 %psum.111 = f32[]{:T(128)} all-reduce(f32[]{:T(128)} %multiply_reduce_fusion.12), channel_id=1, replica_groups=mesh['blk'=16,'rep'=2] {'blk'}, use_global_device_ids=true, to_apply=%region_59.0 | all-reduce | flops 1 | bytes 8 | tf_op jit(solution)/shard_map/psum | solution.py:164
  (424 shorter events, 370.8 us)
Async XLA Ops:
  7.2 264.2 %all-reduce.5.cloned.1.call-start = ((), (), s32[]{:S(2)}) async-start(), calls=%async_computation | async-start | bytes 262144 | tf_op jit(solution)/shard_map/psum | solution.py:131
  7.2 31.1 %collective-permute-start = (f32[3,2048]{1,0:T(4,128)}, f32[3,2048]{1,0:T(4,128)}, u32[]{:S(2)}, u32[]{:S(2)}) collective-permute-start(f32[3,2048]{1,0:T(4,128)} %param.14), channel_id=1, source_target_pairs={{0,30},{2,0},{4,2},{6,4},{8,6},{10,8},{12,10},{14,12},{16,14},{18,... | collective-permute-start | bytes 73736 | tf_op jit(solution)/shard_map/ppermute | solution.py:16
  16.6 21.8 %copy-start.9 = (f32[3,2048]{1,0:T(4,128)S(1)}, f32[3,2048]{1,0:T(4,128)}, u32[]{:S(2)}) copy-start(f32[3,2048]{1,0:T(4,128)} %param.14) | copy-start | bytes 73732
  39.1 4.3 collective-permute-start.1
  44.2 14.1 collective-permute-start.2
  125.0 44.4 %copy-start.42 = (f32[1,6144]{1,0:T(1,128)}, f32[1,6144]{1,0:T(1,128)S(1)}, u32[]{:S(2)}) copy-start(f32[1,6144]{1,0:T(1,128)S(1)} %broadcast.289) | copy-start | bytes 73732
  180.2 9.3 collective-permute-start.3
  191.4 8.2 collective-permute-start.4
  202.0 8.0 collective-permute-start.5
  213.9 35.8 %copy-start.12 = (f32[2048]{0:T(1024)S(1)}, f32[2048]{0:T(1024)}, u32[]{:S(2)}) copy-start(f32[2048]{0:T(1024)} %param.15) | copy-start | bytes 24580
  248.5 759.9 %all-reduce.7.cloned.1.call-start = ((), (), s32[]{:S(2)}) async-start(), calls=%async_computation.1 | async-start | bytes 262144 | tf_op jit(solution)/shard_map/psum | solution.py:131
  273.2 6.9 copy-start.28
  274.6 4.8 collective-permute-start.6
  280.2 28.3 %collective-permute-start.7 = (f32[3,4096]{1,0:T(4,128)}, f32[3,4096]{1,0:T(4,128)}, u32[]{:S(2)}, u32[]{:S(2)}) collective-permute-start(f32[3,4096]{1,0:T(4,128)} %pad_maximum_fusion.14), channel_id=1, source_target_pairs={{0,28},{2,30},{4,0},{6,2},{8,4},{10,6},{12,8},{14,10},{16,12},{18,... | collective-permute-start | bytes 147464 | tf_op jit(solution)/shard_map/ppermute | solution.py:16
  310.0 5.7 collective-permute-start.8
  397.3 7.9 collective-permute-start.9
  406.2 6.8 collective-permute-start.10
  414.3 6.3 collective-permute-start.11
  536.3 1.7 collective-permute-start.12
  538.6 27.2 %collective-permute-start.13 = (f32[3,4096]{1,0:T(4,128)}, f32[3,4096]{1,0:T(4,128)}, u32[]{:S(2)}, u32[]{:S(2)}) collective-permute-start(f32[3,4096]{1,0:T(4,128)} %pad_maximum_fusion.15), channel_id=1, source_target_pairs={{0,28},{2,30},{4,0},{6,2},{8,4},{10,6},{12,8},{14,10},{16,12},{18,... | collective-permute-start | bytes 147464 | tf_op jit(solution)/shard_map/ppermute | solution.py:16
  567.4 9.9 collective-permute-start.14
  659.6 6.6 copy-start.7
  663.3 7.6 collective-permute-start.15
  671.9 6.8 collective-permute-start.16
  678.8 6.0 collective-permute-start.17
  680.8 47.0 %copy-start.18 = (f32[1,2048]{1,0:T(1,128)S(1)}, f32[1,2048]{1,0:T(1,128)}, u32[]{:S(2)}) copy-start(f32[1,2048]{1,0:T(1,128)} %copy-done.17) | copy-start | bytes 24580
  680.8 47.0 %copy-start.24 = (f32[1,2048]{1,0:T(1,128)S(1)}, f32[1,2048]{1,0:T(1,128)}, u32[]{:S(2)}) copy-start(f32[1,2048]{1,0:T(1,128)} %copy-done.23) | copy-start | bytes 24580
  680.8 47.0 %copy-start.26 = (f32[1,2048]{1,0:T(1,128)S(1)}, f32[1,2048]{1,0:T(1,128)}, u32[]{:S(2)}) copy-start(f32[1,2048]{1,0:T(1,128)} %copy-done.25) | copy-start | bytes 24580
  680.8 47.0 %copy-start.51 = (f32[1,2048]{1,0:T(1,128)S(1)}, f32[1,2048]{1,0:T(1,128)}, u32[]{:S(2)}) copy-start(f32[1,2048]{1,0:T(1,128)} %copy-done.50) | copy-start | bytes 24580
  680.8 47.0 %copy-start.53 = (f32[1,2048]{1,0:T(1,128)S(1)}, f32[1,2048]{1,0:T(1,128)}, u32[]{:S(2)}) copy-start(f32[1,2048]{1,0:T(1,128)} %copy-done.52) | copy-start | bytes 24580
  680.8 47.0 %copy-start.59 = (f32[1,2048]{1,0:T(1,128)S(1)}, f32[1,2048]{1,0:T(1,128)}, u32[]{:S(2)}) copy-start(f32[1,2048]{1,0:T(1,128)} %copy-done.58) | copy-start | bytes 24580
  760.1 28.5 %copy-start.10 = (f32[3,2048]{1,0:T(4,128)}, f32[3,2048]{1,0:T(4,128)S(1)}, u32[]{:S(2)}) copy-start(f32[3,2048]{1,0:T(4,128)S(1)} %multiply_add_fusion.3) | copy-start | bytes 73732
  760.1 1.7 collective-permute-start.18
  761.8 23.7 %collective-permute-start.19 = (f32[3,4096]{1,0:T(4,128)S(1)}, f32[3,4096]{1,0:T(4,128)S(1)}, u32[]{:S(2)}, u32[]{:S(2)}) collective-permute-start(f32[3,4096]{1,0:T(4,128)S(1)} %pad_maximum_fusion.16), channel_id=1, source_target_pairs={{0,28},{2,30},{4,0},{6,2},{8,4},{10,6},{12,8},{14,10},{16,12},{18,... | collective-permute-start | bytes 147464 | tf_op jit(solution)/shard_map/ppermute | solution.py:16
  786.2 6.2 collective-permute-start.20
  835.0 11.7 copy-start.44
  837.0 9.7 copy-start.1
  837.0 9.7 copy-start.5
  920.7 9.3 collective-permute-start.21
  922.8 20.9 %copy-start.68 = (f32[6144]{0:T(1024)S(1)}, f32[6144]{0:T(1024)}, u32[]{:S(2)}) copy-start(f32[6144]{0:T(1024)} %get-tuple-element.16) | copy-start | bytes 73732
  931.2 8.0 collective-permute-start.22
  940.7 8.5 collective-permute-start.23
  953.1 56.2 %copy-start.11 = (f32[3,2048]{1,0:T(4,128)S(1)}, f32[3,2048]{1,0:T(4,128)}, u32[]{:S(2)}) copy-start(f32[3,2048]{1,0:T(4,128)} %copy-done.10) | copy-start | bytes 73732
  1009.3 7.8 copy-start.27
  1011.6 4.8 collective-permute-start.24
  1017.2 28.3 %collective-permute-start.25 = (f32[3,4096]{1,0:T(4,128)}, f32[3,4096]{1,0:T(4,128)}, u32[]{:S(2)}, u32[]{:S(2)}) collective-permute-start(f32[3,4096]{1,0:T(4,128)} %pad_maximum_fusion.17), channel_id=1, source_target_pairs={{0,28},{2,30},{4,0},{6,2},{8,4},{10,6},{12,8},{14,10},{16,12},{18,... | collective-permute-start | bytes 147464 | tf_op jit(solution)/shard_map/ppermute | solution.py:16
  1047.0 5.4 collective-permute-start.26
  1134.0 7.9 collective-permute-start.27
  1143.0 6.8 collective-permute-start.28
  1151.1 6.3 collective-permute-start.29
  1273.5 1.7 collective-permute-start.30
  1275.8 27.2 %collective-permute-start.31 = (f32[3,4096]{1,0:T(4,128)}, f32[3,4096]{1,0:T(4,128)}, u32[]{:S(2)}, u32[]{:S(2)}) collective-permute-start(f32[3,4096]{1,0:T(4,128)} %pad_maximum_fusion.18), channel_id=1, source_target_pairs={{0,28},{2,30},{4,0},{6,2},{8,4},{10,6},{12,8},{14,10},{16,12},{18,... | collective-permute-start | bytes 147464 | tf_op jit(solution)/shard_map/ppermute | solution.py:16
  1304.5 9.9 collective-permute-start.32
  1400.4 7.6 collective-permute-start.33
  1409.0 6.8 collective-permute-start.34
  1415.9 6.0 collective-permute-start.35
  1417.9 47.0 %copy-start.16 = (f32[1,2048]{1,0:T(1,128)S(1)}, f32[1,2048]{1,0:T(1,128)}, u32[]{:S(2)}) copy-start(f32[1,2048]{1,0:T(1,128)} %copy-done.15) | copy-start | bytes 24580
  1417.9 47.0 %copy-start.20 = (f32[1,2048]{1,0:T(1,128)S(1)}, f32[1,2048]{1,0:T(1,128)}, u32[]{:S(2)}) copy-start(f32[1,2048]{1,0:T(1,128)} %copy-done.19) | copy-start | bytes 24580
  1417.9 47.0 %copy-start.22 = (f32[1,2048]{1,0:T(1,128)S(1)}, f32[1,2048]{1,0:T(1,128)}, u32[]{:S(2)}) copy-start(f32[1,2048]{1,0:T(1,128)} %copy-done.21) | copy-start | bytes 24580
  1417.9 47.0 %copy-start.47 = (f32[1,2048]{1,0:T(1,128)S(1)}, f32[1,2048]{1,0:T(1,128)}, u32[]{:S(2)}) copy-start(f32[1,2048]{1,0:T(1,128)} %copy-done.46) | copy-start | bytes 24580
  1418.0 47.0 %copy-start.49 = (f32[1,2048]{1,0:T(1,128)S(1)}, f32[1,2048]{1,0:T(1,128)}, u32[]{:S(2)}) copy-start(f32[1,2048]{1,0:T(1,128)} %copy-done.48) | copy-start | bytes 24580
  1418.0 47.0 %copy-start.55 = (f32[1,2048]{1,0:T(1,128)S(1)}, f32[1,2048]{1,0:T(1,128)}, u32[]{:S(2)}) copy-start(f32[1,2048]{1,0:T(1,128)} %copy-done.54) | copy-start | bytes 24580
  1418.0 47.6 %copy-start.45 = (f32[8,768]{1,0:T(8,128)S(1)}, f32[8,768]{1,0:T(8,128)}, u32[]{:S(2)}) copy-start(f32[8,768]{1,0:T(8,128)} %copy-done.44) | copy-start | bytes 73732
  1418.0 47.6 %copy-start.73 = (s32[1,8,1]{1,2,0:T(1,128)S(1)}, s32[1,8,1]{1,2,0:T(1,128)}, u32[]{:S(2)}) copy-start(s32[1,8,1]{1,2,0:T(1,128)} %param.13) | copy-start | bytes 100
  (48 other events, 145.7 us)
Sparse Core Ops, SparseCore 0:
  248.6 22.7 all-reduce.4
  987.8 20.5 all-reduce.6
where the time goes:
time: 1510 us
  local copies, waits for them, and re-layouts  571 us (38%)
  other arithmetic  551 us (36%)
  blocking collectives  215 us (14%)
  waiting for transfers between devices  93.6 us (6%)
  starting transfers between devices  51.1 us (3%)
  between operations  23.4 us (2%)
    scatter-add x12, other arithmetic, spread(): jax.ops.segment_sum(values, index, num_segments=total)  408 us
    gather x12, local copies, waits for them, and re-layouts, on_device(): changed = window[:, second] - rotate(rotation, direction[:, first])  197 us
    psum x4, blocking collectives, precond_sum(): return lax.psum(jnp.sum(residual * scaled), 'blk')  121 us
    unnamed x174, local copies, waits for them, and re-layouts  61.6 us
    psum x2, blocking collectives, on_device(): step_size = norm_now / lax.psum(jnp.sum(direction * image), 'blk')  60.4 us
    ppermute x36, waiting for transfers between devices, shifted(): return lax.ppermute(value, axis, pairs)  52.6 us
    ppermute x36, starting transfers between devices, shifted(): return lax.ppermute(value, axis, pairs)  51 us
    gather x2, local copies, waits for them, and re-layouts, on_device(): window[:, second] - rotate(rotation, estimate[:, first])  48.6 us
  transfers between devices with their start and end apart: 38, of which 21 were waited for; matrix products, arithmetic and copies ran while one was open for 18% of the time, Pallas kernels for 0%

commit v1 on v0

--- a/solution.py
+++ b/solution.py
@@ -128,7 +128,10 @@
         return current[:, 0]
 
     def reduce_halves(sums):
-        return lax.psum(sums, "rep")
+        hold_sectors = lambda local_values: jax.lax.all_gather(local_values, axis_name="rep").sum(
+            axis=0
+        )
+        return hold_sectors(sums)
 
     def collect(far_terms, near_terms):
         channels = far_terms.shape[0]

time: 1510 us -> 1460 us (0.967)
  waiting for transfers between devices: 93.6 us -> 46.7 us
    psum x2 -> x0, waiting for transfers between devices: 40.9 us -> none  [reduce_halves(): return lax.psum(sums, 'rep')]
    psum x4 -> x0, blocking collectives: 33.9 us -> none  [reduce_halves(): return lax.psum(sums, 'rep')]
    all_gather x0 -> x6, blocking collectives: none -> 33.6 us  [reduce_halves(): jax.lax.all_gather(local_values, axis_name='rep').sum(axis=0)]
    unnamed x174 -> x180, local copies, waits for them, and re-layouts: 61.6 us -> 70.9 us
  transfers between devices with their start and end apart: 38 -> 36, of which waited for: 21 -> 19; matrix products, arithmetic and copies ran while one was open for 18% -> 18% of each run, Pallas kernels for 0% -> 0%
where the time goes in v1:
time: 1460 us; the launch traced here: 1450 us
  local copies, waits for them, and re-layouts  571 us (39%)
  other arithmetic  558 us (38%)
  blocking collectives  216 us (15%)
  starting transfers between devices  51.9 us (4%)
  waiting for transfers between devices  46.7 us (3%)
    scatter-add x12, other arithmetic, spread(): jax.ops.segment_sum(values, index, num_segments=total)  408 us
    gather x12, local copies, waits for them, and re-layouts, on_device(): changed = window[:, second] - rotate(rotation, direction[:, first])  197 us
    psum x4, blocking collectives, precond_sum(): return lax.psum(jnp.sum(residual * scaled), 'blk')  122 us
    unnamed x180, local copies, waits for them, and re-layouts  70.9 us
    psum x2, blocking collectives, on_device(): step_size = norm_now / lax.psum(jnp.sum(direction * image), 'blk')  60.2 us
    ppermute x36, starting transfers between devices, shifted(): return lax.ppermute(value, axis, pairs)  51.9 us
    gather x2, local copies, waits for them, and re-layouts, on_device(): window[:, second] - rotate(rotation, estimate[:, first])  48.6 us
    slice x18, local copies, waits for them, and re-layouts, returned(): moved = shifted(current[:, half_width:width], 'blk', half_width)  47.8 us
  transfers between devices with their start and end apart: 36, of which 19 were waited for; matrix products, arithmetic and copies ran while one was open for 18% of the time, Pallas kernels for 0%

profile of v1, /device:TPU:0, one launch (start us, length us, event | category | flops | bytes accessed | tf_op | source)
XLA Modules:
  0.0 1453.1 jit_solution(4037688807136227678)
XLA Ops:
  0.6 5.5 collective-permute-start
  10.0 17.3 %gather_fusion.1 = f32[6144,3]{1,0:T(8,128)S(1)} fusion(f32[3,2048]{0,1:T(8,128)} %copy.819, s32[6144]{0:T(1024)S(1)} %broadcast_clamp_fusion), kind=kCustom, calls=%fused_computation.1 | custom fusion | bytes 172032 | tf_op jit(solution)/shard_map/gather | solution.py:149
  52.5 5.1 copy.818
  57.6 24.3 %gather_fusion = f32[6144,3]{1,0:T(8,128)} fusion(f32[3,16384]{0,1:T(8,128)} %copy.818, s32[6144]{0:T(1024)S(1)} %broadcast_clamp_fusion.1), kind=kCustom, calls=%fused_computation | custom fusion | bytes 172032 | tf_op jit(solution)/shard_map/gather | solution.py:149
  89.3 9.5 fusion.12
  98.8 5.4 fusion.44
  125.4 37.4 %scatter_custom_fusion = f32[9,16384]{0,1:T(8,128)} fusion(s32[6144]{0:T(1024)} %bitcast.247, f32[6144,9]{1,0:T(8,128)} %copy.829, f32[]{:T(128)} %constant.7.clone.1), kind=kCustom, calls=%fused_computation.39 | custom fusion | flops 55296 | bytes 590336 | tf_op jit(solution)/shard_map/vmap()/scatter-add | solution.py:85
  162.8 7.4 fusion.42
  178.7 4.2 collective-permute-done.3
  184.8 4.7 collective-permute-start.4
  207.4 32.3 %scatter_fusion = f32[9,2048]{0,1:T(8,128)} fusion(f32[9,2048]{0,1:T(8,128)} %bitcast.197, s32[6144]{0:T(1024)S(1)} %reshape.813, f32[6144,9]{1,0:T(8,128)} %copy.837), kind=kCustom, calls=%fused_computation.13 | custom fusion | flops 55296 | bytes 688128 | tf_op jit(solution)/shard_map/vmap()/scatter-add | solution.py:85
  241.9 6.9 all-gather.6
  261.8 22.1 %gather_fusion.3 = f32[6144,3]{1,0:T(8,128)} fusion(f32[3,2048]{0,1:T(8,128)} %copy.840, s32[6144]{0:T(1024)S(1)} %broadcast_clamp_fusion), kind=kCustom, calls=%fused_computation.3 | custom fusion | bytes 172032 | tf_op jit(solution)/shard_map/gather | solution.py:164
  295.4 5.7 copy.839
  301.0 24.3 %gather_fusion.2 = f32[6144,3]{1,0:T(8,128)} fusion(f32[3,16384]{0,1:T(8,128)} %copy.839, s32[6144]{0:T(1024)S(1)} %broadcast_clamp_fusion.1), kind=kCustom, calls=%fused_computation.2 | custom fusion | bytes 172032 | tf_op jit(solution)/shard_map/gather | solution.py:164
  325.3 5.0 fusion.21
  330.3 34.2 %scatter_custom_fusion.2 = f32[3,16384]{0,1:T(8,128)} fusion(s32[6144]{0:T(1024)} %bitcast.248, f32[]{:T(128)} %constant.7.clone.1, f32[3,6144]{0,1:T(8,128)} %fusion.21), kind=kCustom, calls=%fused_computation.35 | custom fusion | flops 18432 | bytes 3342848 | tf_op jit(solution)/shard_map/vmap()/scatter-add | solution.py:85
  364.5 7.4 fusion.41
  387.7 3.8 collective-permute-done.10
  402.8 32.3 %scatter_fusion.1 = f32[3,2048]{0,1:T(8,128)} fusion(f32[3,2048]{0,1:T(8,128)} %bitcast.203, s32[6144]{0:T(1024)S(1)} %reshape.813, f32[6144,3]{1,0:T(8,128)} %copy.847), kind=kCustom, calls=%fused_computation.15 | custom fusion | flops 18432 | bytes 245760 | tf_op jit(solution)/shard_map/vmap()/scatter-add | solution.py:85
  437.2 4.9 all-gather.7
  445.1 30.7 %all-reduce.1 = (f32[]{:T(128)}, f32[]{:T(128)}) all-reduce(f32[]{:T(128)} %get-tuple-element.31, f32[]{:T(128)} %get-tuple-element.30), channel_id=1, replica_groups=mesh['blk'=16,'rep'=2] {'blk'}, use_global_device_ids=true, to_apply=%region_13.0 | all-reduce | flops 2 | bytes 16 | tf_op jit(solution)/shard_map/psum | solution.py:143
  481.0 30.1 %psum.58 = f32[]{:T(128)} all-reduce(f32[]{:T(128)} %multiply_reduce_fusion.17), channel_id=1, replica_groups=mesh['blk'=16,'rep'=2] {'blk'}, use_global_device_ids=true, to_apply=%region_22.0 | all-reduce | flops 1 | bytes 8 | tf_op jit(solution)/shard_map/psum | solution.py:143
  517.6 22.1 %gather_fusion.5 = f32[6144,3]{1,0:T(8,128)} fusion(f32[3,2048]{0,1:T(8,128)} %copy.849, s32[6144]{0:T(1024)S(1)} %broadcast_clamp_fusion), kind=kCustom, calls=%fused_computation.5 | custom fusion | bytes 172032 | tf_op jit(solution)/shard_map/gather | solution.py:164
  557.6 8.2 pad_maximum_fusion
  565.7 24.3 %gather_fusion.4 = f32[6144,3]{1,0:T(8,128)} fusion(f32[3,16384]{0,1:T(8,128)} %pad_maximum_fusion, s32[6144]{0:T(1024)S(1)} %broadcast_clamp_fusion.1), kind=kCustom, calls=%fused_computation.4 | custom fusion | bytes 172032 | tf_op jit(solution)/shard_map/gather | solution.py:164
  590.0 5.0 fusion.19
  595.0 34.2 %scatter_custom_fusion.4 = f32[3,16384]{0,1:T(8,128)} fusion(s32[6144]{0:T(1024)} %bitcast.249, f32[]{:T(128)} %constant.7.clone.1, f32[3,6144]{0,1:T(8,128)} %fusion.19), kind=kCustom, calls=%fused_computation.33 | custom fusion | flops 18432 | bytes 3342848 | tf_op jit(solution)/shard_map/vmap()/scatter-add | solution.py:85
  629.2 7.4 fusion.40
  650.0 5.6 collective-permute-done.16
  662.1 33.9 %scatter_fusion.2 = f32[3,2048]{0,1:T(8,128)S(1)} fusion(f32[3,2048]{0,1:T(8,128)S(1)} %bitcast.205, s32[6144]{0:T(1024)S(1)} %reshape.813, f32[6144,3]{1,0:T(8,128)} %copy.860), kind=kCustom, calls=%fused_computation.17 | custom fusion | flops 18432 | bytes 245760 | tf_op jit(solution)/shard_map/vmap()/scatter-add | solution.py:85
  696.3 4.6 all-gather.8
  701.6 30.1 %psum.59 = f32[]{:T(128)} all-reduce(f32[]{:T(128)} %multiply_reduce_fusion.16), channel_id=1, replica_groups=mesh['blk'=16,'rep'=2] {'blk'}, use_global_device_ids=true, to_apply=%region_29.0 | all-reduce | flops 1 | bytes 8 | tf_op jit(solution)/shard_map/psum | solution.py:167
  735.4 20.9 %gather_fusion.7 = f32[6144,3]{1,0:T(8,128)} fusion(f32[3,2048]{0,1:T(8,128)S(1)} %copy.862, s32[6144]{0:T(1024)S(1)} %broadcast_clamp_fusion), kind=kCustom, calls=%fused_computation.7 | custom fusion | bytes 172032 | tf_op jit(solution)/shard_map/gather | solution.py:149
  769.0 8.9 pad_maximum_fusion.1
  777.9 24.3 %gather_fusion.6 = f32[6144,3]{1,0:T(8,128)} fusion(f32[3,16384]{0,1:T(8,128)} %pad_maximum_fusion.1, s32[6144]{0:T(1024)S(1)} %broadcast_clamp_fusion.1), kind=kCustom, calls=%fused_computation.6 | custom fusion | bytes 172032 | tf_op jit(solution)/shard_map/gather | solution.py:149
  810.2 9.7 fusion.13
  822.0 5.2 fusion.43
  845.8 37.2 %scatter_custom_fusion.6 = f32[9,16384]{0,1:T(8,128)} fusion(s32[6144]{0:T(1024)} %bitcast.250, f32[6144,9]{1,0:T(8,128)} %copy.874, f32[]{:T(128)} %constant.7.clone.1), kind=kCustom, calls=%fused_computation.37 | custom fusion | flops 55296 | bytes 590336 | tf_op jit(solution)/shard_map/vmap()/scatter-add | solution.py:85
  883.0 7.4 fusion.39
  904.4 3.8 collective-permute-start.22
  908.2 4.2 collective-permute-done.22
  926.3 32.3 %scatter_fusion.3 = f32[9,2048]{0,1:T(8,128)} fusion(f32[9,2048]{0,1:T(8,128)} %bitcast.199, s32[6144]{0:T(1024)S(1)} %reshape.813, f32[6144,9]{1,0:T(8,128)} %copy.879), kind=kCustom, calls=%fused_computation.19 | custom fusion | flops 55296 | bytes 688128 | tf_op jit(solution)/shard_map/vmap()/scatter-add | solution.py:85
  960.8 7.7 all-gather.9
  979.5 22.1 %gather_fusion.9 = f32[6144,3]{1,0:T(8,128)} fusion(f32[3,2048]{0,1:T(8,128)} %copy.882, s32[6144]{0:T(1024)S(1)} %broadcast_clamp_fusion), kind=kCustom, calls=%fused_computation.9 | custom fusion | bytes 172032 | tf_op jit(solution)/shard_map/gather | solution.py:164
  1013.9 5.7 copy.881
  1019.5 24.3 %gather_fusion.8 = f32[6144,3]{1,0:T(8,128)} fusion(f32[3,16384]{0,1:T(8,128)} %copy.881, s32[6144]{0:T(1024)S(1)} %broadcast_clamp_fusion.1), kind=kCustom, calls=%fused_computation.8 | custom fusion | bytes 172032 | tf_op jit(solution)/shard_map/gather | solution.py:164
  1043.8 5.0 fusion.17
  1048.8 34.2 %scatter_custom_fusion.8 = f32[3,16384]{0,1:T(8,128)} fusion(s32[6144]{0:T(1024)} %bitcast.251, f32[]{:T(128)} %constant.7.clone.1, f32[3,6144]{0,1:T(8,128)} %fusion.17), kind=kCustom, calls=%fused_computation.31 | custom fusion | flops 18432 | bytes 3342848 | tf_op jit(solution)/shard_map/vmap()/scatter-add | solution.py:85
  1083.0 7.4 fusion.38
  1120.5 32.3 %scatter_fusion.4 = f32[3,2048]{0,1:T(8,128)} fusion(f32[3,2048]{0,1:T(8,128)} %bitcast.207, s32[6144]{0:T(1024)S(1)} %reshape.813, f32[6144,3]{1,0:T(8,128)} %copy.889), kind=kCustom, calls=%fused_computation.21 | custom fusion | flops 18432 | bytes 245760 | tf_op jit(solution)/shard_map/vmap()/scatter-add | solution.py:85
  1154.9 4.9 all-gather.10
  1162.8 30.9 %all-reduce = (f32[]{:T(128)}, f32[]{:T(128)}) all-reduce(f32[]{:T(128)} %get-tuple-element.29, f32[]{:T(128)} %get-tuple-element.28), channel_id=1, replica_groups=mesh['blk'=16,'rep'=2] {'blk'}, use_global_device_ids=true, to_apply=%region_43.0 | all-reduce | flops 2 | bytes 16 | tf_op jit(solution)/shard_map/psum | solution.py:143
  1199.1 30.2 %psum.62 = f32[]{:T(128)} all-reduce(f32[]{:T(128)} %multiply_reduce_fusion.13), channel_id=1, replica_groups=mesh['blk'=16,'rep'=2] {'blk'}, use_global_device_ids=true, to_apply=%region_52.0 | all-reduce | flops 1 | bytes 8 | tf_op jit(solution)/shard_map/psum | solution.py:143
  1236.0 22.1 %gather_fusion.11 = f32[6144,3]{1,0:T(8,128)} fusion(f32[3,2048]{0,1:T(8,128)} %copy.891, s32[6144]{0:T(1024)S(1)} %broadcast_clamp_fusion), kind=kCustom, calls=%fused_computation.11 | custom fusion | bytes 172032 | tf_op jit(solution)/shard_map/gather | solution.py:164
  1276.0 8.2 pad_maximum_fusion.2
  1284.1 24.3 %gather_fusion.10 = f32[6144,3]{1,0:T(8,128)} fusion(f32[3,16384]{0,1:T(8,128)} %pad_maximum_fusion.2, s32[6144]{0:T(1024)S(1)} %broadcast_clamp_fusion.1), kind=kCustom, calls=%fused_computation.10 | custom fusion | bytes 172032 | tf_op jit(solution)/shard_map/gather | solution.py:164
  1308.4 5.0 fusion.15
  1313.3 34.2 %scatter_custom_fusion.10 = f32[3,16384]{0,1:T(8,128)} fusion(s32[6144]{0:T(1024)} %bitcast.252, f32[]{:T(128)} %constant.7.clone.1, f32[3,6144]{0,1:T(8,128)} %fusion.15), kind=kCustom, calls=%fused_computation.29 | custom fusion | flops 18432 | bytes 3342848 | tf_op jit(solution)/shard_map/vmap()/scatter-add | solution.py:85
  1347.6 7.4 fusion.37
  1368.4 5.6 collective-permute-done.34
  1380.4 33.9 %scatter_fusion.5 = f32[3,2048]{0,1:T(8,128)S(1)} fusion(f32[3,2048]{0,1:T(8,128)S(1)} %bitcast.201, s32[6144]{0:T(1024)S(1)} %reshape.813, f32[6144,3]{1,0:T(8,128)} %copy.902), kind=kCustom, calls=%fused_computation.23 | custom fusion | flops 18432 | bytes 245760 | tf_op jit(solution)/shard_map/vmap()/scatter-add | solution.py:85
  1414.7 4.6 all-gather.11
  1420.7 30.1 %psum.63 = f32[]{:T(128)} all-reduce(f32[]{:T(128)} %multiply_reduce_fusion.12), channel_id=1, replica_groups=mesh['blk'=16,'rep'=2] {'blk'}, use_global_device_ids=true, to_apply=%region_59.0 | all-reduce | flops 1 | bytes 8 | tf_op jit(solution)/shard_map/psum | solution.py:167
  (426 shorter events, 374.0 us)
Async XLA Ops:
  0.6 31.1 %collective-permute-start = (f32[3,2048]{1,0:T(4,128)}, f32[3,2048]{1,0:T(4,128)}, u32[]{:S(2)}, u32[]{:S(2)}) collective-permute-start(f32[3,2048]{1,0:T(4,128)} %param.14), channel_id=1, source_target_pairs={{0,30},{2,0},{4,2},{6,4},{8,6},{10,8},{12,10},{14,12},{16,14},{18,... | collective-permute-start | bytes 73736 | tf_op jit(solution)/shard_map/ppermute | solution.py:16
  10.0 21.8 %copy-start.9 = (f32[3,2048]{1,0:T(4,128)S(1)}, f32[3,2048]{1,0:T(4,128)}, u32[]{:S(2)}) copy-start(f32[3,2048]{1,0:T(4,128)} %param.14) | copy-start | bytes 73732
  32.6 4.3 collective-permute-start.1
  37.7 14.1 collective-permute-start.2
  118.4 44.4 %copy-start.42 = (f32[1,6144]{1,0:T(1,128)}, f32[1,6144]{1,0:T(1,128)S(1)}, u32[]{:S(2)}) copy-start(f32[1,6144]{1,0:T(1,128)S(1)} %broadcast.289) | copy-start | bytes 73732
  173.7 17.8 %copy-start.12 = (f32[2048]{0:T(1024)S(1)}, f32[2048]{0:T(1024)}, u32[]{:S(2)}) copy-start(f32[2048]{0:T(1024)} %param.15) | copy-start | bytes 24580
  173.7 9.3 collective-permute-start.3
  184.8 8.2 collective-permute-start.4
  195.5 8.0 collective-permute-start.5
  252.3 7.3 copy-start.28
  253.0 6.6 copy-start.56
  253.0 6.6 copy-start.63
  253.7 5.2 collective-permute-start.6
  259.6 27.3 %collective-permute-start.7 = (f32[3,4096]{1,0:T(4,128)}, f32[3,4096]{1,0:T(4,128)}, u32[]{:S(2)}, u32[]{:S(2)}) collective-permute-start(f32[3,4096]{1,0:T(4,128)} %pad_maximum_fusion.14), channel_id=1, source_target_pairs={{0,28},{2,30},{4,0},{6,2},{8,4},{10,6},{12,8},{14,10},{16,12},{18,... | collective-permute-start | bytes 147464 | tf_op jit(solution)/shard_map/ppermute | solution.py:16
  288.4 5.3 collective-permute-start.8
  375.3 8.3 collective-permute-start.9
  384.6 6.8 collective-permute-start.10
  392.8 6.5 collective-permute-start.11
  513.2 1.7 collective-permute-start.12
  515.5 27.2 %collective-permute-start.13 = (f32[3,4096]{1,0:T(4,128)}, f32[3,4096]{1,0:T(4,128)}, u32[]{:S(2)}, u32[]{:S(2)}) collective-permute-start(f32[3,4096]{1,0:T(4,128)} %pad_maximum_fusion.15), channel_id=1, source_target_pairs={{0,28},{2,30},{4,0},{6,2},{8,4},{10,6},{12,8},{14,10},{16,12},{18,... | collective-permute-start | bytes 147464 | tf_op jit(solution)/shard_map/ppermute | solution.py:16
  544.3 9.9 collective-permute-start.14
  636.5 6.6 copy-start.7
  640.2 7.6 collective-permute-start.15
  648.8 6.8 collective-permute-start.16
  655.7 6.0 collective-permute-start.17
  657.7 43.2 %copy-start.18 = (f32[1,2048]{1,0:T(1,128)S(1)}, f32[1,2048]{1,0:T(1,128)}, u32[]{:S(2)}) copy-start(f32[1,2048]{1,0:T(1,128)} %copy-done.17) | copy-start | bytes 24580
  657.7 43.2 %copy-start.24 = (f32[1,2048]{1,0:T(1,128)S(1)}, f32[1,2048]{1,0:T(1,128)}, u32[]{:S(2)}) copy-start(f32[1,2048]{1,0:T(1,128)} %copy-done.23) | copy-start | bytes 24580
  657.7 43.2 %copy-start.26 = (f32[1,2048]{1,0:T(1,128)S(1)}, f32[1,2048]{1,0:T(1,128)}, u32[]{:S(2)}) copy-start(f32[1,2048]{1,0:T(1,128)} %copy-done.25) | copy-start | bytes 24580
  657.7 43.2 %copy-start.51 = (f32[1,2048]{1,0:T(1,128)S(1)}, f32[1,2048]{1,0:T(1,128)}, u32[]{:S(2)}) copy-start(f32[1,2048]{1,0:T(1,128)} %copy-done.50) | copy-start | bytes 24580
  657.7 43.2 %copy-start.53 = (f32[1,2048]{1,0:T(1,128)S(1)}, f32[1,2048]{1,0:T(1,128)}, u32[]{:S(2)}) copy-start(f32[1,2048]{1,0:T(1,128)} %copy-done.52) | copy-start | bytes 24580
  657.7 43.2 %copy-start.59 = (f32[1,2048]{1,0:T(1,128)S(1)}, f32[1,2048]{1,0:T(1,128)}, u32[]{:S(2)}) copy-start(f32[1,2048]{1,0:T(1,128)} %copy-done.58) | copy-start | bytes 24580
  733.1 28.8 %copy-start.10 = (f32[3,2048]{1,0:T(4,128)}, f32[3,2048]{1,0:T(4,128)S(1)}, u32[]{:S(2)}) copy-start(f32[3,2048]{1,0:T(4,128)S(1)} %multiply_add_fusion.3) | copy-start | bytes 73732
  733.1 1.9 collective-permute-start.18
  735.0 23.7 %collective-permute-start.19 = (f32[3,4096]{1,0:T(4,128)S(1)}, f32[3,4096]{1,0:T(4,128)S(1)}, u32[]{:S(2)}, u32[]{:S(2)}) collective-permute-start(f32[3,4096]{1,0:T(4,128)S(1)} %pad_maximum_fusion.16), channel_id=1, source_target_pairs={{0,28},{2,30},{4,0},{6,2},{8,4},{10,6},{12,8},{14,10},{16,12},{18,... | collective-permute-start | bytes 147464 | tf_op jit(solution)/shard_map/ppermute | solution.py:16
  759.4 6.2 collective-permute-start.20
  808.1 11.7 copy-start.44
  810.2 9.7 copy-start.1
  810.2 9.7 copy-start.5
  893.9 9.3 collective-permute-start.21
  895.9 20.9 %copy-start.68 = (f32[6144]{0:T(1024)S(1)}, f32[6144]{0:T(1024)}, u32[]{:S(2)}) copy-start(f32[6144]{0:T(1024)} %get-tuple-element.16) | copy-start | bytes 73732
  904.4 8.0 collective-permute-start.22
  913.9 8.6 collective-permute-start.23
  926.3 44.8 %copy-start.11 = (f32[3,2048]{1,0:T(4,128)S(1)}, f32[3,2048]{1,0:T(4,128)}, u32[]{:S(2)}) copy-start(f32[3,2048]{1,0:T(4,128)} %copy-done.10) | copy-start | bytes 73732
  973.4 3.2 collective-permute-start.24
  977.3 27.3 %collective-permute-start.25 = (f32[3,4096]{1,0:T(4,128)}, f32[3,4096]{1,0:T(4,128)}, u32[]{:S(2)}, u32[]{:S(2)}) collective-permute-start(f32[3,4096]{1,0:T(4,128)} %pad_maximum_fusion.17), channel_id=1, source_target_pairs={{0,28},{2,30},{4,0},{6,2},{8,4},{10,6},{12,8},{14,10},{16,12},{18,... | collective-permute-start | bytes 147464 | tf_op jit(solution)/shard_map/ppermute | solution.py:16
  1006.1 6.1 collective-permute-start.26
  1093.8 7.8 collective-permute-start.27
  1102.6 6.8 collective-permute-start.28
  1110.7 6.3 collective-permute-start.29
  1231.6 1.7 collective-permute-start.30
  1233.9 27.2 %collective-permute-start.31 = (f32[3,4096]{1,0:T(4,128)}, f32[3,4096]{1,0:T(4,128)}, u32[]{:S(2)}, u32[]{:S(2)}) collective-permute-start(f32[3,4096]{1,0:T(4,128)} %pad_maximum_fusion.18), channel_id=1, source_target_pairs={{0,28},{2,30},{4,0},{6,2},{8,4},{10,6},{12,8},{14,10},{16,12},{18,... | collective-permute-start | bytes 147464 | tf_op jit(solution)/shard_map/ppermute | solution.py:16
  1262.6 9.9 collective-permute-start.32
  1354.9 6.6 copy-start.6
  1358.5 7.6 collective-permute-start.33
  1367.1 6.8 collective-permute-start.34
  1374.0 6.0 collective-permute-start.35
  1376.0 43.2 %copy-start.16 = (f32[1,2048]{1,0:T(1,128)S(1)}, f32[1,2048]{1,0:T(1,128)}, u32[]{:S(2)}) copy-start(f32[1,2048]{1,0:T(1,128)} %copy-done.15) | copy-start | bytes 24580
  1376.0 43.2 %copy-start.20 = (f32[1,2048]{1,0:T(1,128)S(1)}, f32[1,2048]{1,0:T(1,128)}, u32[]{:S(2)}) copy-start(f32[1,2048]{1,0:T(1,128)} %copy-done.19) | copy-start | bytes 24580
  1376.0 43.2 %copy-start.22 = (f32[1,2048]{1,0:T(1,128)S(1)}, f32[1,2048]{1,0:T(1,128)}, u32[]{:S(2)}) copy-start(f32[1,2048]{1,0:T(1,128)} %copy-done.21) | copy-start | bytes 24580
  1376.1 43.2 %copy-start.47 = (f32[1,2048]{1,0:T(1,128)S(1)}, f32[1,2048]{1,0:T(1,128)}, u32[]{:S(2)}) copy-start(f32[1,2048]{1,0:T(1,128)} %copy-done.46) | copy-start | bytes 24580
  1376.1 43.2 %copy-start.49 = (f32[1,2048]{1,0:T(1,128)S(1)}, f32[1,2048]{1,0:T(1,128)}, u32[]{:S(2)}) copy-start(f32[1,2048]{1,0:T(1,128)} %copy-done.48) | copy-start | bytes 24580
  1376.1 43.2 %copy-start.55 = (f32[1,2048]{1,0:T(1,128)S(1)}, f32[1,2048]{1,0:T(1,128)}, u32[]{:S(2)}) copy-start(f32[1,2048]{1,0:T(1,128)} %copy-done.54) | copy-start | bytes 24580
  1376.1 43.9 %copy-start.45 = (f32[8,768]{1,0:T(8,128)S(1)}, f32[8,768]{1,0:T(8,128)}, u32[]{:S(2)}) copy-start(f32[8,768]{1,0:T(8,128)} %copy-done.44) | copy-start | bytes 73732
  1376.1 43.9 %copy-start.73 = (s32[1,8,1]{1,2,0:T(1,128)S(1)}, s32[1,8,1]{1,2,0:T(1,128)}, u32[]{:S(2)}) copy-start(s32[1,8,1]{1,2,0:T(1,128)} %param.13) | copy-start | bytes 100
  (46 other events, 124.2 us)
